TPU v7x, 32 devices: a whole 2x2x4 slice. The times are simulated.
32 devices in a mesh: expert: 4 (over z), shard: 8 (over y, x, core).
Axes of the slice: x: 2, y: 2, z: 4, core: 2. Of those that a mesh axis runs over, the one named last changes fastest.
Arguments:
- master_down: float32 [16, 6400, 4096], P('expert', None, 'shard'), may hold values from -0.109375 to 0.109375
- second_down: bfloat16 [16, 6400, 4096], P('expert', None, 'shard'), may hold values from -0.0390625 to 0.0390625
- router_weight: float32 [4096, 16], P('shard', 'expert'), may hold values from -0.09375 to 0.09375
- router_gain: float32 [4096], P('shard'), may hold values from 0.25 to 1.75
Outputs:
- final_down: bfloat16 [16, 6400, 4096], P('expert', 'shard')
- scale_down: float32 [16, 6400], P('expert', 'shard')
- serve_router: bfloat16 [4096, 16], replicated
All inputs are finite; a program needn't handle non-finite values.
Results may differ from a plain program's by a relative error of at most 0.001.
Values may be sent and summed in bfloat16 or wider, within the bound.
No kernel may reach another device: no remote copies, remote signals or barrier semaphores. Data moves between devices by JAX's collectives and lax.ppermute only.
A program may use at most 256 MiB of HBM per device.

v0:
```python
import jax
import jax.numpy as jnp
from jax import lax
from jax.sharding import PartitionSpec as P


def local(master_down, second_down, router_weight, router_gain):
    merged_down = master_down + second_down.astype(jnp.float32)
    total_down = lax.psum(jnp.sum(merged_down * merged_down, axis=2), "shard")
    scale_down = jnp.sqrt(total_down)
    narrow_down = (merged_down / jnp.expand_dims(scale_down, 2)).astype(jnp.bfloat16)
    final_down = lax.all_to_all(narrow_down, "shard", split_axis=1, concat_axis=2, tiled=True)
    scale_down = lax.dynamic_slice_in_dim(
        scale_down, lax.axis_index("shard") * final_down.shape[1], final_down.shape[1], axis=1
    )
    part_router = (router_weight * router_gain[:, None]).astype(jnp.bfloat16)
    row_router = lax.all_gather(part_router, "shard", axis=0, tiled=True)
    serve_router = lax.all_gather(row_router, "expert", axis=1, tiled=True)
    return (final_down, scale_down, serve_router)


def solution(mesh):
    return jax.shard_map(
        local,
        mesh=mesh,
        in_specs=(
            P("expert", None, "shard"),
            P("expert", None, "shard"),
            P("shard", "expert"),
            P("shard"),
        ),
        out_specs=(P("expert", "shard", None), P("expert", "shard"), P()),
        check_vma=False,
    )
```

profile of v0, /device:TPU:0, one launch (start us, length us, event | category | flops | bytes accessed | tf_op | source)
XLA Modules:
  0.0 554.8 jit_solution(7517493062815123618)
XLA Ops:
  7.2 0.0 all-reduce.2.cloned.1.call-start
  7.2 24.2 %multiply_reduce_fusion = f32[4,6400]{1,0:T(4,128)S(1)} fusion(f32[4,6400,512]{2,1,0:T(8,128)} %param.4, bf16[4,6400,512]{2,1,0:T(8,128)(2,1)} %param.5), kind=kLoop, calls=%fused_computation.1 | loop fusion | flops 52403200 | bytes 78745600 | tf_op jit(solution)/shard_map/reduce_sum | solution.py:9
  31.4 2.3 copy.21
  33.7 0.0 all-reduce.2.cloned.1.call-update
  33.7 73.6 %all-reduce.2.cloned.1.call-done = f32[4,6400]{0,1:T(8,128)} async-done(((f32[4,6400]{0,1:T(8,128)}), f32[4,6400]{0,1:T(8,128)}) %all-reduce.2.cloned.1.call-update) | async-done | bytes 102416 | tf_op jit(solution)/shard_map/psum | solution.py:9
  107.3 2.7 sqrt.3
  110.0 1.2 copy.17
  111.3 34.3 %divide_convert_fusion = bf16[4,6400,512]{2,1,0:T(8,128)(2,1)} fusion(f32[4,6400,512]{2,1,0:T(8,128)} %param.4, bf16[4,6400,512]{2,1,0:T(8,128)(2,1)} %param.5, f32[4,6400]{1,0:T(4,128)S(1)} %copy.17), kind=kLoop, calls=%fused_computation | loop fusion | flops 52428800 | bytes 104960000 | tf_op jit(solution)/shard_map/convert_element_type | solution.py:11
  145.5 33.4 %copy.18 = bf16[4,6400,512]{2,0,1:T(4,128)(2,1)} copy(bf16[4,6400,512]{2,1,0:T(8,128)(2,1)} %divide_convert_fusion) | data formatting | bytes 52428800 | tf_op jit(solution)/shard_map/convert_element_type | solution.py:11
  178.9 0.0 copy-start
  178.9 0.0 copy-start.1
  178.9 6.6 %all-to-all-start = ((bf16[4,6400,512]{2,0,1:T(4,128)(2,1)}), bf16[4,6400,512]{2,0,1:T(4,128)(2,1)}, u32[]{:S(2)}, u32[]{:S(2)}) async-start(bf16[4,6400,512]{2,0,1:T(4,128)(2,1)} %copy.18), calls=%async_computation | async-start | bytes 52428800 | tf_op jit(solution)/shard_map/all_to_all | solution.py:12
  185.6 0.0 copy-done
  185.6 0.0 copy-done.1
  185.6 288.2 %all_gather.6 = bf16[4096,4]{0,1:T(4,128)(2,1)S(1)} all-gather(bf16[512,4]{0,1:T(4,128)(2,1)S(1)} %multiply_convert_fusion), channel_id=1, replica_groups=mesh['expert'=4,'shard'=8] {'shard'}, dimensions={0}, use_global_device_ids=true | all-gather | bytes 36864 | tf_op jit(solution)/shard_map/all_gather | solution.py:17
  473.8 13.5 %all-gather = bf16[4,4,4096]{2,1,0:T(4,128)(2,1)S(1)} all-gather(bf16[1,4,4096]{2,1,0:T(4,128)(2,1)S(1)} %bitcast.9), channel_id=1, replica_groups=mesh['expert'=4,'shard'=8] {'expert'}, dimensions={0}, use_global_device_ids=true | all-gather | bytes 163840 | tf_op jit(solution)/shard_map/all_gather | solution.py:18
  487.3 0.7 reshape.9
  488.0 0.8 constant_dynamic-slice_fusion
  488.7 1.8 copy.20
  490.5 0.0 all-to-all-done
  490.5 18.2 %copy.19 = bf16[4,800,8,512]{3,2,1,0:T(8,128)(2,1)} copy(bf16[4,800,8,512]{3,0,1,2:T(4,128)(2,1)} %bitcast.1) | data formatting | bytes 52428800 | tf_op jit(solution)/shard_map/all_to_all | solution.py:12
  508.7 39.2 %all_to_all.16 = bf16[4,800,4096]{2,1,0:T(8,128)(2,1)} reshape(bf16[4,800,8,512]{3,2,1,0:T(8,128)(2,1)} %copy.19) | data formatting | bytes 52428800 | tf_op jit(solution)/shard_map/all_to_all | solution.py:12
  (1 shorter events, 0.0 us)
Async XLA Ops:
  7.2 100.2 %all-reduce.2.cloned.1.call-start = ((), (), s32[]{:S(2)}) async-start(), calls=%async_computation.1 | async-start | bytes 6553600 | tf_op jit(solution)/shard_map/psum | solution.py:9
  178.9 6.7 %copy-start = (f32[512,4]{0,1:T(4,128)S(1)}, f32[512,4]{0,1:T(4,128)}, u32[]{:S(2)}) copy-start(f32[512,4]{0,1:T(4,128)} %param.6) | copy-start | bytes 24580
  178.9 6.7 %copy-start.1 = (f32[512]{0:T(512)S(1)}, f32[512]{0:T(512)}, u32[]{:S(2)}) copy-start(f32[512]{0:T(512)} %param.7) | copy-start | bytes 6148
  178.9 311.6 %all-to-all-start = ((bf16[4,6400,512]{2,0,1:T(4,128)(2,1)}), bf16[4,6400,512]{2,0,1:T(4,128)(2,1)}, u32[]{:S(2)}, u32[]{:S(2)}) async-start(bf16[4,6400,512]{2,0,1:T(4,128)(2,1)} %copy.18), calls=%async_computation | async-start | bytes 52428800 | tf_op jit(solution)/shard_map/all_to_all | solution.py:12
Sparse Core Ops, SparseCore 0:
  33.9 73.4 all-reduce.1
where the time goes:
time: 556 us; the launch traced here: 555 us
  blocking collectives  302 us (54%)
  local copies, waits for them, and re-layouts  100 us (18%)
  waiting for transfers between devices  73.6 us (13%)
  other arithmetic  58.5 us (11%)
  between operations  14.1 us (3%)
  starting transfers between devices  6.67 us (1%)
    all_gather x1, blocking collectives, local(): row_router = lax.all_gather(part_router, 'shard', axis=0, tiled=True)  288 us
    psum x1, waiting for transfers between devices, local(): total_down = lax.psum(jnp.sum(merged_down * merged_down, axis=2), 'shard')  73.6 us
    all_to_all x2, local copies, waits for them, and re-layouts, local(): lax.all_to_all(narrow_down, 'shard', split_axis=1, concat_axis=2, tiled=T...  57.4 us
    convert_element_type x1, other arithmetic, local(): (merged_down / jnp.expand_dims(scale_down, 2)).astype(jnp.bfloat16)  34.3 us
    convert_element_type x1, local copies, waits for them, and re-layouts, local(): (merged_down / jnp.expand_dims(scale_down, 2)).astype(jnp.bfloat16)  33.4 us
    reduce_sum x1, other arithmetic, local(): total_down = lax.psum(jnp.sum(merged_down * merged_down, axis=2), 'shard')  24.2 us
    all_gather x1, blocking collectives, local(): serve_router = lax.all_gather(row_router, 'expert', axis=1, tiled=True)  13.5 us
  transfers between devices with their start and end apart: 2, of which 1 were waited for; matrix products, arithmetic and copies ran while one was open for 1% of the time, Pallas kernels for 0%

commit v1 on v0

v1 whole, which is shorter than its diff:
```python
import jax
import jax.numpy as jnp
from jax import lax
from jax.experimental import pallas as pl
from jax.experimental.pallas import tpu as pltpu
from jax.sharding import PartitionSpec as P


def row_block(rows):
    return max(d for d in range(1, 101) if rows % d == 0 and (d % 16 == 0 or d == rows or d == 1))


def place(me, parts, whole, e, low, block, shape):
    n = len(parts)
    rows, width = parts[0].shape
    first = whole is None

    def body(me_ref, *refs):
        out_ref = refs[-1]
        for k in range(n):
            column = pl.multiple_of((me_ref[0] ^ k) * width, width)
            out_ref[0, :, pl.ds(column, width)] = refs[k][...]

    return pl.pallas_call(
        body,
        out_shape=jax.ShapeDtypeStruct(shape, parts[0].dtype),
        grid_spec=pltpu.PrefetchScalarGridSpec(
            num_scalar_prefetch=1,
            grid=(rows // block,),
            in_specs=[pl.BlockSpec((block, width), lambda r, _: (r, 0))] * n
            + ([] if first else [pl.BlockSpec(memory_space=pl.ANY)]),
            out_specs=pl.BlockSpec((1, block, n * width), lambda r, _: (e, low // block + r, 0)),
        ),
        input_output_aliases={} if first else {1 + n: 0},
    )(me, *parts, *([] if first else [whole]))


def send_order(n):
    return [k for k in sorted(range(1, n), key=lambda k: (k & 1, k)) if k != 1] + [1]


def after(values, earlier):
    return lax.optimization_barrier((values, earlier))[0]


def local(master_down, second_down, router_weight, router_gain):
    experts, rows, width = master_down.shape
    n = lax.axis_size("shard")
    me = lax.axis_index("shard")
    own_rows = rows // n
    block = row_block(own_rows)
    order = send_order(n)
    early, late = order[: n // 2], order[n // 2 :]

    def swap(x, k, axis="shard"):
        return lax.ppermute(x, axis, [(i, i ^ k) for i in range(lax.axis_size(axis))])

    def squares(pair, low, high):
        m = pair[0][low:high] + pair[1][low:high].astype(jnp.float32)
        return jnp.sum(m * m, axis=2)

    def narrow(pair, scale, e, k, low, high):
        start = (me ^ k) * own_rows + low
        cut = lambda x: lax.dynamic_slice(x, (e, start, 0), (1, high - low, width))[0]
        m = cut(pair[0]) + cut(pair[1]).astype(jnp.float32)
        return (m / lax.dynamic_slice_in_dim(scale, start, high - low)[:, None]).astype(jnp.bfloat16)

    pair = (master_down, second_down)
    sums = squares(pair, 0, 1)
    scale = jnp.sqrt(jnp.sum(lax.all_gather(sums, "shard", axis=0), axis=0))[0]
    parts = [None] * n
    pair, scale0 = after((pair, scale), scale)
    for k in early:
        piece = narrow(pair, scale0, 0, k, 0, own_rows)
        parts[k] = swap(piece, k)
        pair, scale0 = after((pair, scale0), piece)

    sums = squares(pair, 1, experts)
    router = (router_weight * router_gain[:, None]).T
    cols, dim = router.shape
    mixed = jnp.concatenate([sums.reshape(-1), router.reshape(-1)])
    pair, scale0 = after((pair, scale0), mixed)
    mixes = [mixed] + [swap(mixed, k) for k in range(1, n)]
    for k in late:
        piece = narrow(pair, scale0, 0, k, 0, own_rows)
        parts[k] = swap(piece, k)
        pair, scale0 = after((pair, scale0), piece)
    parts[0] = narrow(pair, scale0, 0, 0, 0, own_rows)
    rest = mixes[0][: sums.size]
    for mix in mixes[1:]:
        rest = rest + mix[: sums.size]
    rest = jnp.sqrt(rest).reshape(sums.shape)
    wide = jnp.zeros((cols, dim * n), jnp.bfloat16)
    for k, mix in enumerate(mixes):
        got = mix[sums.size :].reshape(cols, dim).astype(jnp.bfloat16)
        wide = lax.dynamic_update_slice(wide, got, (0, (me ^ k) * dim))
    scales = [scale] + [rest[e] for e in range(experts - 1)]

    shape = (experts, own_rows, n * width)
    where = jnp.reshape(me, (1,)).astype(jnp.int32)
    chunks = [(e, 0, own_rows) for e in range(1, experts - 1)]
    chunks += [(experts - 1, 0, own_rows - 2 * block), (experts - 1, own_rows - 2 * block, own_rows)]
    arrived = [(parts, 0, 0)]
    for e, low, high in chunks:
        pair, scale = after((pair, scales[e]), scales[e])
        parts, pieces = [None] * n, []
        for group in ([order[:2], order[2:4], order[4:] + [0]] if e == 1 else [order + [0]]):
            for k in group:
                pieces.append(narrow(pair, scale, e, k, low, high))
                parts[k] = swap(pieces[-1], k) if k else pieces[-1]
            pair = after(pair, pieces)
        arrived.append((parts, e, low))
    wide = after(wide, pieces)
    whole = None
    for parts, e, low in arrived:
        whole = place(where, parts, whole, e, low, block, shape)

    m = lax.axis_size("expert")
    mine = lax.axis_index("expert")
    tall = jnp.zeros((cols * m, dim * n), jnp.bfloat16)
    for k in range(m):
        tall = lax.dynamic_update_slice(tall, swap(wide, k, "expert") if k else wide, ((mine ^ k) * cols, 0))

    scale_down = jnp.stack([lax.dynamic_slice_in_dim(s, me * own_rows, own_rows) for s in scales])
    return (whole, scale_down, tall.T)


def solution(mesh):
    return jax.shard_map(
        local,
        mesh=mesh,
        in_specs=(
            P("expert", None, "shard"),
            P("expert", None, "shard"),
            P("shard", "expert"),
            P("shard"),
        ),
        out_specs=(P("expert", "shard", None), P("expert", "shard"), P()),
        check_vma=False,
    )
```

time: 556 us -> 439 us (0.79)
  blocking collectives: 302 us -> 10.8 us
  waiting for transfers between devices: 73.6 us -> 238 us
  local copies, waits for them, and re-layouts: 100 us -> 19.6 us
  starting transfers between devices: 6.67 us -> 46.2 us
  Pallas kernels: 0 us -> 36.3 us
  other arithmetic: 58.5 us -> 83.5 us
  between operations: 14.1 us -> 1.44 us
    all_gather x2 -> x1, blocking collectives: 302 us -> 10.8 us  [local(): scale = jnp.sqrt(jnp.sum(lax.all_gather(sums, 'shard', axis=0), axis=0))[0]]
    ppermute x0 -> x45, waiting for transfers between devices: none -> 238 us  [swap(): lax.ppermute(x, axis, [(i, i ^ k) for i in range(lax.axis_size(axis))])]
    psum x1 -> x0, waiting for transfers between devices: 73.6 us -> none  [local(): total_down = lax.psum(jnp.sum(merged_down * merged_down, axis=2), 'shard')]
    all_to_all x2 -> x0, local copies, waits for them, and re-layouts: 57.4 us -> none  [local(): lax.all_to_all(narrow_down, 'shard', split_axis=1, concat_axis=2, tiled=T...]
    ppermute x0 -> x45, starting transfers between devices: none -> 46.2 us  [swap(): lax.ppermute(x, axis, [(i, i ^ k) for i in range(lax.axis_size(axis))])]
    pallas_call x0 -> x5, Pallas kernels: none -> 36.3 us  [place(): pl.pallas_call(body, out_shape=jax.ShapeDtypeStruct(shape, parts[0].dtype...]
    convert_element_type x1 -> x7, local copies, waits for them, and re-layouts: 33.4 us -> 4.22 us  [local(): got = mix[sums.size:].reshape(cols, dim).astype(jnp.bfloat16)]
    convert_element_type x2 -> x14, other arithmetic: 34.3 us -> 53.1 us  [narrow(): (m / lax.dynamic_slice_in_dim(scale, start, high - low)[:, None]).astype(...]
  transfers between devices with their start and end apart: 2 -> 45, of which waited for: 1 -> 23; matrix products, arithmetic and copies ran while one was open for 1% -> 6% of each run, Pallas kernels for 0% -> 8%
where the time goes in v1:
time: 439 us; the launch traced here: 436 us
  waiting for transfers between devices  238 us (54%)
  other arithmetic  83.5 us (19%)
  starting transfers between devices  46.2 us (11%)
  Pallas kernels  36.3 us (8%)
  local copies, waits for them, and re-layouts  19.6 us (4%)
  blocking collectives  10.8 us (2%)
    ppermute x45, waiting for transfers between devices, swap(): lax.ppermute(x, axis, [(i, i ^ k) for i in range(lax.axis_size(axis))])  238 us
    convert_element_type x14, other arithmetic, narrow(): (m / lax.dynamic_slice_in_dim(scale, start, high - low)[:, None]).astype(...  53.1 us
    ppermute x45, starting transfers between devices, swap(): lax.ppermute(x, axis, [(i, i ^ k) for i in range(lax.axis_size(axis))])  46.2 us
    pallas_call x5, Pallas kernels, place(): pl.pallas_call(body, out_shape=jax.ShapeDtypeStruct(shape, parts[0].dtype...  36.3 us
    reduce_sum x2, other arithmetic, squares(): return jnp.sum(m * m, axis=2)  27.7 us
    all_gather x1, blocking collectives, local(): scale = jnp.sqrt(jnp.sum(lax.all_gather(sums, 'shard', axis=0), axis=0))[0]  10.8 us
  transfers between devices with their start and end apart: 45, of which 23 were waited for; matrix products, arithmetic and copies ran while one was open for 6% of the time, Pallas kernels for 8%

profile of v1, /device:TPU:0, one launch (start us, length us, event | category | flops | bytes accessed | tf_op | source)
XLA Modules:
  0.0 436.1 jit_solution(61417984427210021)
XLA Ops:
  1.4 8.4 %multiply_reduce_fusion.1 = f32[6400]{0:T(1024)S(1)} fusion(f32[4,6400,512]{2,1,0:T(8,128)} %param.4, bf16[4,6400,512]{2,1,0:T(8,128)(2,1)} %param.5), kind=kLoop, calls=%fused_computation.1 | loop fusion | flops 13100800 | bytes 19686400 | tf_op jit(solution)/shard_map/reduce_sum | solution.py:60
  9.8 10.8 %all-gather.1 = f32[8,1,6400]{2,1,0:T(1,128)S(1)} all-gather(f32[1,1,6400]{2,1,0:T(1,128)S(1)} %reshape.179), channel_id=2, replica_groups=mesh['expert'=4,'shard'=8] {'shard'}, dimensions={0}, use_global_device_ids=true | all-gather | bytes 230400 | tf_op jit(solution)/shard_map/all_gather | solution.py:70
  28.5 19.3 %multiply_reduce_fusion = f32[3,6400]{1,0:T(4,128)S(1)} fusion(f32[4,6400,512]{2,1,0:T(8,128)} %param.4, bf16[4,6400,512]{2,1,0:T(8,128)(2,1)} %param.5), kind=kLoop, calls=%fused_computation | loop fusion | flops 39302400 | bytes 59059200 | tf_op jit(solution)/shard_map/reduce_sum | solution.py:60
  84.7 5.6 %fusion.9 = (bf16[800,512]{1,0:T(8,128)(2,1)}, bf16[800,512]{1,0:T(8,128)(2,1)}, bf16[800,512]{1,0:T(8,128)(2,1)}, bf16[800,512]{1,0:T(8,128)(2,1)}) fusion(f32[4,6400,512]{2,1,0:T(8,128)} %param.4, s32[]{:T(128)S(6)} %select_n.63, f32[800]{0:T(1024)S(1)} %get-tuple-element.162, bf16[4,6400,512]{2,1,0:T(8,128)(2,1)} %param.5, ...), kind=kLoop, calls=%fused_computation.21 | loop fusion | flops 6553600 | bytes 13120016 | tf_op jit(solution)/shard_map/convert_element_type | solution.py:66
  90.5 10.4 %fusion.1 = (bf16[800,512]{1,0:T(8,128)(2,1)}, bf16[800,512]{1,0:T(8,128)(2,1)}, bf16[800,512]{1,0:T(8,128)(2,1)}, bf16[800,512]{1,0:T(8,128)(2,1)}, bf16[800,51...) fusion(f32[4,6400,512]{2,1,0:T(8,128)} %param.4, ...), kind=kLoop, calls=%fused_computation.5 | loop fusion | flops 13107200 | bytes 26240032 | tf_op jit(solution)/shard_map/convert_element_type | solution.py:66
  101.0 7.0 %fusion.24 = (bf16[640,512]{1,0:T(8,128)(2,1)}, bf16[640,512]{1,0:T(8,128)(2,1)S(1)}, bf16[640,512]{1,0:T(8,128)(2,1)S(1)}, bf16[640,512]{1,0:T(8,128)(2,1)S(1)}...) fusion(f32[4,6400,512]{2,1,0:T(8,128)} %param.4, ...), kind=kLoop, calls=%fused_computation.51 | loop fusion | flops 10485760 | bytes 20992032 | tf_op jit(solution)/shard_map/convert_element_type | solution.py:66
  139.2 8.2 %collective-permute-done.18.refs_5_ = bf16[640,512]{1,0:T(8,128)(2,1)S(1)} collective-permute-done((bf16[640,512]{1,0:T(8,128)(2,1)S(1)}, bf16[640,512]{1,0:T(8,128)(2,1)S(1)}, u32[]{:S(2)}, u32[]{:S(2)}) %collective-permute-start.18) | collective-permute-done | bytes 655392 | tf_op jit(solution)/shard_map/ppermute | solution.py:56
  154.1 14.0 %collective-permute-done.19.refs_6_ = bf16[640,512]{1,0:T(8,128)(2,1)} collective-permute-done((bf16[640,512]{1,0:T(8,128)(2,1)S(1)}, bf16[640,512]{1,0:T(8,128)(2,1)}, u32[]{:S(2)}, u32[]{:S(2)}) %collective-permute-start.19) | collective-permute-done | bytes 655392 | tf_op jit(solution)/shard_map/ppermute | solution.py:56
  169.0 6.6 %collective-permute-done.17.refs_4_ = bf16[640,512]{1,0:T(8,128)(2,1)} collective-permute-done((bf16[640,512]{1,0:T(8,128)(2,1)S(1)}, bf16[640,512]{1,0:T(8,128)(2,1)}, u32[]{:S(2)}, u32[]{:S(2)}) %collective-permute-start.17) | collective-permute-done | bytes 655392 | tf_op jit(solution)/shard_map/ppermute | solution.py:56
  184.1 15.7 %collective-permute-done.41.refs_7_ = bf16[800,512]{1,0:T(8,128)(2,1)S(1)} collective-permute-done((bf16[800,512]{1,0:T(8,128)(2,1)S(1)}, bf16[800,512]{1,0:T(8,128)(2,1)S(1)}, u32[]{:S(2)}, u32[]{:S(2)}) %collective-permute-start.41) | collective-permute-done | bytes 819232 | tf_op jit(solution)/shard_map/ppermute | solution.py:56
  201.1 9.4 %collective-permute-done.39.refs_5_ = bf16[800,512]{1,0:T(8,128)(2,1)S(1)} collective-permute-done((bf16[800,512]{1,0:T(8,128)(2,1)S(1)}, bf16[800,512]{1,0:T(8,128)(2,1)S(1)}, u32[]{:S(2)}, u32[]{:S(2)}) %collective-permute-start.39) | collective-permute-done | bytes 819232 | tf_op jit(solution)/shard_map/ppermute | solution.py:56
  217.9 16.8 %collective-permute-done.40.refs_6_ = bf16[800,512]{1,0:T(8,128)(2,1)S(1)} collective-permute-done((bf16[800,512]{1,0:T(8,128)(2,1)S(1)}, bf16[800,512]{1,0:T(8,128)(2,1)S(1)}, u32[]{:S(2)}, u32[]{:S(2)}) %collective-permute-start.40) | collective-permute-done | bytes 819232 | tf_op jit(solution)/shard_map/ppermute | solution.py:56
  235.7 10.1 %collective-permute-done.38.refs_4_ = bf16[800,512]{1,0:T(8,128)(2,1)S(1)} collective-permute-done((bf16[800,512]{1,0:T(8,128)(2,1)S(1)}, bf16[800,512]{1,0:T(8,128)(2,1)S(1)}, u32[]{:S(2)}, u32[]{:S(2)}) %collective-permute-start.38) | collective-permute-done | bytes 819232 | tf_op jit(solution)/shard_map/ppermute | solution.py:56
  252.6 10.8 %collective-permute-done.31.refs_4_ = bf16[800,512]{1,0:T(8,128)(2,1)} collective-permute-done((bf16[800,512]{1,0:T(8,128)(2,1)}, bf16[800,512]{1,0:T(8,128)(2,1)}, u32[]{:S(2)}, u32[]{:S(2)}) %collective-permute-start.31) | collective-permute-done | bytes 819232 | tf_op jit(solution)/shard_map/ppermute | solution.py:56
  270.2 17.4 %collective-permute-done.30.refs_3_ = bf16[800,512]{1,0:T(8,128)(2,1)} collective-permute-done((bf16[800,512]{1,0:T(8,128)(2,1)}, bf16[800,512]{1,0:T(8,128)(2,1)}, u32[]{:S(2)}, u32[]{:S(2)}) %collective-permute-start.30) | collective-permute-done | bytes 819232 | tf_op jit(solution)/shard_map/ppermute | solution.py:56
  287.6 17.5 %collective-permute-done.33.refs_6_ = bf16[800,512]{1,0:T(8,128)(2,1)} collective-permute-done((bf16[800,512]{1,0:T(8,128)(2,1)}, bf16[800,512]{1,0:T(8,128)(2,1)}, u32[]{:S(2)}, u32[]{:S(2)}) %collective-permute-start.33) | collective-permute-done | bytes 819232 | tf_op jit(solution)/shard_map/ppermute | solution.py:56
  310.3 12.6 %collective-permute-done.34.refs_7_ = bf16[800,512]{1,0:T(8,128)(2,1)S(1)} collective-permute-done((bf16[800,512]{1,0:T(8,128)(2,1)}, bf16[800,512]{1,0:T(8,128)(2,1)S(1)}, u32[]{:S(2)}, u32[]{:S(2)}) %collective-permute-start.34) | collective-permute-done | bytes 819232 | tf_op jit(solution)/shard_map/ppermute | solution.py:56
  322.9 19.0 %collective-permute-done.32.refs_5_ = bf16[800,512]{1,0:T(8,128)(2,1)S(1)} collective-permute-done((bf16[800,512]{1,0:T(8,128)(2,1)}, bf16[800,512]{1,0:T(8,128)(2,1)S(1)}, u32[]{:S(2)}, u32[]{:S(2)}) %collective-permute-start.32) | collective-permute-done | bytes 819232 | tf_op jit(solution)/shard_map/ppermute | solution.py:56
  346.3 30.6 %collective-permute-done.25.refs_5_ = bf16[800,512]{1,0:T(8,128)(2,1)S(1)} collective-permute-done((bf16[800,512]{1,0:T(8,128)(2,1)}, bf16[800,512]{1,0:T(8,128)(2,1)S(1)}, u32[]{:S(2)}, u32[]{:S(2)}) %collective-permute-start.25) | collective-permute-done | bytes 819232 | tf_op jit(solution)/shard_map/ppermute | solution.py:56
  380.3 15.8 %collective-permute-done.24.refs_4_ = bf16[800,512]{1,0:T(8,128)(2,1)S(1)} collective-permute-done((bf16[800,512]{1,0:T(8,128)(2,1)S(1)}, bf16[800,512]{1,0:T(8,128)(2,1)S(1)}, u32[]{:S(2)}, u32[]{:S(2)}) %collective-permute-start.24) | collective-permute-done | bytes 819232 | tf_op jit(solution)/shard_map/ppermute | solution.py:56
  398.4 8.9 %shard_map.67.refs_8_ = bf16[4,800,4096]{2,1,0:T(8,128)(2,1)} custom-call(s32[1]{0:T(128)} %bitcast.me_ref, bf16[800,512]{1,0:T(8,128)(2,1)} %fusion.refs_0_, bf16[800,512]{1,0:T(8,128)(2,1)} %copy-done.7, bf16[800,512]{1,0:T(8,128)(2,1)} %collective-permute-done.36.refs_2_, bf16[800,512]{1,0:T(8,128)(2,1)} %copy-done.10, bf16[800,512]{1,0:T(8,128)(2,1)} %copy-done.12, ...), custom_call_target="tpu_custom_call" | custom-call | tf_op jit(solution)/shard_map/pallas_call | solution.py:24
  407.3 8.9 %shard_map.68.refs_8_ = bf16[4,800,4096]{2,1,0:T(8,128)(2,1)} custom-call(s32[1]{0:T(128)} %bitcast.me_ref, bf16[800,512]{1,0:T(8,128)(2,1)} %get-tuple-element.127.refs_0_, bf16[800,512]{1,0:T(8,128)(2,1)} %copy-done.13, bf16[800,512]{1,0:T(8,128)(2,1)} %collective-permute-done.29.refs_2_, ...), custom_call_target="tpu_custom_call", output_to_operand_aliasing={{}: (9, {})} | custom-call | tf_op jit(solution)/shard_map/pallas_call | solution.py:24
  416.2 8.9 %shard_map.69.refs_8_ = bf16[4,800,4096]{2,1,0:T(8,128)(2,1)} custom-call(s32[1]{0:T(128)} %bitcast.me_ref, bf16[800,512]{1,0:T(8,128)(2,1)} %get-tuple-element.119.refs_0_, bf16[800,512]{1,0:T(8,128)(2,1)} %copy-done.16, bf16[800,512]{1,0:T(8,128)(2,1)} %copy-done.22, bf16[800,512]{1,0:T(8,128)(2,1)} %copy-done.19, ...), custom_call_target="tpu_custom_call", output_to_operand_aliasing={{}: (9, {})} | custom-call | tf_op jit(solution)/shard_map/pallas_call | solution.py:24
  425.1 7.3 %shard_map.70.refs_8_ = bf16[4,800,4096]{2,1,0:T(8,128)(2,1)} custom-call(s32[1]{0:T(128)} %bitcast.me_ref, bf16[640,512]{1,0:T(8,128)(2,1)} %get-tuple-element.111.refs_0_, bf16[640,512]{1,0:T(8,128)(2,1)} %copy-done.23, bf16[640,512]{1,0:T(8,128)(2,1)} %collective-permute-done.15.refs_2_, ...), custom_call_target="tpu_custom_call", output_to_operand_aliasing={{}: (9, {})} | custom-call | tf_op jit(solution)/shard_map/pallas_call | solution.py:24
  (250 shorter events, 134.5 us)
Async XLA Ops:
  132.1 50.1 %collective-permute-start.35 = (bf16[800,512]{1,0:T(8,128)(2,1)S(1)}, bf16[800,512]{1,0:T(8,128)(2,1)S(1)}, u32[]{:S(2)}, u32[]{:S(2)}) collective-permute-start(bf16[800,512]{1,0:T(8,128)(2,1)S(1)} %copy-done.2), channel_id=1, source_target_pairs={{0,1},{1,0},{2,3},{3,2},{4,5},{5,4},{6,7},{7,6},{8,9},{9,8},{10,11... | collective-permute-start | bytes 2457608 | tf_op jit(solution)/shard_map/ppermute | solution.py:56
  154.1 45.8 %collective-permute-start.41 = (bf16[800,512]{1,0:T(8,128)(2,1)S(1)}, bf16[800,512]{1,0:T(8,128)(2,1)S(1)}, u32[]{:S(2)}, u32[]{:S(2)}) collective-permute-start(bf16[800,512]{1,0:T(8,128)(2,1)S(1)} %copy-done.1), channel_id=1, source_target_pairs={{0,7},{1,6},{2,5},{3,4},{4,3},{5,2},{6,1},{7,0},{8,15},{9,14},{10,... | collective-permute-start | bytes 2457608 | tf_op jit(solution)/shard_map/ppermute | solution.py:56
  168.1 42.5 %collective-permute-start.39 = (bf16[800,512]{1,0:T(8,128)(2,1)S(1)}, bf16[800,512]{1,0:T(8,128)(2,1)S(1)}, u32[]{:S(2)}, u32[]{:S(2)}) collective-permute-start(bf16[800,512]{1,0:T(8,128)(2,1)S(1)} %copy-done), channel_id=1, source_target_pairs={{0,5},{1,4},{2,7},{3,6},{4,1},{5,0},{6,3},{7,2},{8,13},{9,12},{10,... | collective-permute-start | bytes 2457608 | tf_op jit(solution)/shard_map/ppermute | solution.py:56
  175.7 41.6 %collective-permute-start.37 = (bf16[800,512]{1,0:T(8,128)(2,1)S(1)}, bf16[800,512]{1,0:T(8,128)(2,1)S(1)}, u32[]{:S(2)}, u32[]{:S(2)}) collective-permute-start(bf16[800,512]{1,0:T(8,128)(2,1)S(1)} %fusion.20), channel_id=1, source_target_pairs={{0,3},{1,2},{2,1},{3,0},{4,7},{5,6},{6,5},{7,4},{8,11},{9,10},{10,... | collective-permute-start | bytes 2457608 | tf_op jit(solution)/shard_map/ppermute | solution.py:56
  180.7 54.1 %collective-permute-start.40 = (bf16[800,512]{1,0:T(8,128)(2,1)S(1)}, bf16[800,512]{1,0:T(8,128)(2,1)S(1)}, u32[]{:S(2)}, u32[]{:S(2)}) collective-permute-start(bf16[800,512]{1,0:T(8,128)(2,1)S(1)} %fusion.21), channel_id=1, source_target_pairs={{0,6},{1,7},{2,4},{3,5},{4,2},{5,3},{6,0},{7,1},{8,14},{9,15},{10,... | collective-permute-start | bytes 2457608 | tf_op jit(solution)/shard_map/ppermute | solution.py:56
  182.2 63.6 %collective-permute-start.38 = (bf16[800,512]{1,0:T(8,128)(2,1)S(1)}, bf16[800,512]{1,0:T(8,128)(2,1)S(1)}, u32[]{:S(2)}, u32[]{:S(2)}) collective-permute-start(bf16[800,512]{1,0:T(8,128)(2,1)S(1)} %fusion.22), channel_id=1, source_target_pairs={{0,4},{1,5},{2,6},{3,7},{4,0},{5,1},{6,2},{7,3},{8,12},{9,13},{10,... | collective-permute-start | bytes 2457608 | tf_op jit(solution)/shard_map/ppermute | solution.py:56
  199.8 51.2 %collective-permute-start.36 = (bf16[800,512]{1,0:T(8,128)(2,1)S(1)}, bf16[800,512]{1,0:T(8,128)(2,1)}, u32[]{:S(2)}, u32[]{:S(2)}) collective-permute-start(bf16[800,512]{1,0:T(8,128)(2,1)S(1)} %fusion.23), channel_id=1, source_target_pairs={{0,2},{1,3},{2,0},{3,1},{4,6},{5,7},{6,4},{7,5},{8,10},{9,11},{10,... | collective-permute-start | bytes 2457608 | tf_op jit(solution)/shard_map/ppermute | solution.py:56
  210.6 52.8 %collective-permute-start.31 = (bf16[800,512]{1,0:T(8,128)(2,1)}, bf16[800,512]{1,0:T(8,128)(2,1)}, u32[]{:S(2)}, u32[]{:S(2)}) collective-permute-start(bf16[800,512]{1,0:T(8,128)(2,1)} %get-tuple-element.133), channel_id=1, source_target_pairs={{0,4},{1,5},{2,6},{3,7},{4,0},{5,1},{6,2},{7,3},{8,12},{9,13},{10,... | collective-permute-start | bytes 2457608 | tf_op jit(solution)/shard_map/ppermute | solution.py:56
  217.2 51.3 %collective-permute-start.29 = (bf16[800,512]{1,0:T(8,128)(2,1)}, bf16[800,512]{1,0:T(8,128)(2,1)}, u32[]{:S(2)}, u32[]{:S(2)}) collective-permute-start(bf16[800,512]{1,0:T(8,128)(2,1)} %get-tuple-element.134), channel_id=1, source_target_pairs={{0,2},{1,3},{2,0},{3,1},{4,6},{5,7},{6,4},{7,5},{8,10},{9,11},{10,... | collective-permute-start | bytes 2457608 | tf_op jit(solution)/shard_map/ppermute | solution.py:56
  234.8 52.8 %collective-permute-start.30 = (bf16[800,512]{1,0:T(8,128)(2,1)}, bf16[800,512]{1,0:T(8,128)(2,1)}, u32[]{:S(2)}, u32[]{:S(2)}) collective-permute-start(bf16[800,512]{1,0:T(8,128)(2,1)} %get-tuple-element.131), channel_id=1, source_target_pairs={{0,3},{1,2},{2,1},{3,0},{4,7},{5,6},{6,5},{7,4},{8,11},{9,10},{10,... | collective-permute-start | bytes 2457608 | tf_op jit(solution)/shard_map/ppermute | solution.py:56
  246.8 58.4 %collective-permute-start.33 = (bf16[800,512]{1,0:T(8,128)(2,1)}, bf16[800,512]{1,0:T(8,128)(2,1)}, u32[]{:S(2)}, u32[]{:S(2)}) collective-permute-start(bf16[800,512]{1,0:T(8,128)(2,1)} %get-tuple-element.132), channel_id=1, source_target_pairs={{0,6},{1,7},{2,4},{3,5},{4,2},{5,3},{6,0},{7,1},{8,14},{9,15},{10,... | collective-permute-start | bytes 2457608 | tf_op jit(solution)/shard_map/ppermute | solution.py:56
  251.0 59.0 %collective-permute-start.28 = (bf16[800,512]{1,0:T(8,128)(2,1)}, bf16[800,512]{1,0:T(8,128)(2,1)S(1)}, u32[]{:S(2)}, u32[]{:S(2)}) collective-permute-start(bf16[800,512]{1,0:T(8,128)(2,1)} %get-tuple-element.128), channel_id=1, source_target_pairs={{0,1},{1,0},{2,3},{3,2},{4,5},{5,4},{6,7},{7,6},{8,9},{9,8},{10,11... | collective-permute-start | bytes 2457608 | tf_op jit(solution)/shard_map/ppermute | solution.py:56
  263.4 59.4 %collective-permute-start.34 = (bf16[800,512]{1,0:T(8,128)(2,1)}, bf16[800,512]{1,0:T(8,128)(2,1)S(1)}, u32[]{:S(2)}, u32[]{:S(2)}) collective-permute-start(bf16[800,512]{1,0:T(8,128)(2,1)} %get-tuple-element.129), channel_id=1, source_target_pairs={{0,7},{1,6},{2,5},{3,4},{4,3},{5,2},{6,1},{7,0},{8,15},{9,14},{10,... | collective-permute-start | bytes 2457608 | tf_op jit(solution)/shard_map/ppermute | solution.py:56
  268.6 73.3 %collective-permute-start.32 = (bf16[800,512]{1,0:T(8,128)(2,1)}, bf16[800,512]{1,0:T(8,128)(2,1)S(1)}, u32[]{:S(2)}, u32[]{:S(2)}) collective-permute-start(bf16[800,512]{1,0:T(8,128)(2,1)} %get-tuple-element.130), channel_id=1, source_target_pairs={{0,5},{1,4},{2,7},{3,6},{4,1},{5,0},{6,3},{7,2},{8,13},{9,12},{10,... | collective-permute-start | bytes 2457608 | tf_op jit(solution)/shard_map/ppermute | solution.py:56
  287.6 55.7 %collective-permute-start.21 = (bf16[800,512]{1,0:T(8,128)(2,1)}, bf16[800,512]{1,0:T(8,128)(2,1)S(1)}, u32[]{:S(2)}, u32[]{:S(2)}) collective-permute-start(bf16[800,512]{1,0:T(8,128)(2,1)} %get-tuple-element.120), channel_id=1, source_target_pairs={{0,1},{1,0},{2,3},{3,2},{4,5},{5,4},{6,7},{7,6},{8,9},{9,8},{10,11... | collective-permute-start | bytes 2457608 | tf_op jit(solution)/shard_map/ppermute | solution.py:56
  305.2 40.0 %collective-permute-start.27 = (bf16[800,512]{1,0:T(8,128)(2,1)}, bf16[800,512]{1,0:T(8,128)(2,1)S(1)}, u32[]{:S(2)}, u32[]{:S(2)}) collective-permute-start(bf16[800,512]{1,0:T(8,128)(2,1)} %get-tuple-element.121), channel_id=1, source_target_pairs={{0,7},{1,6},{2,5},{3,4},{4,3},{5,2},{6,1},{7,0},{8,15},{9,14},{10,... | collective-permute-start | bytes 2457608 | tf_op jit(solution)/shard_map/ppermute | solution.py:56
  310.1 66.9 %collective-permute-start.25 = (bf16[800,512]{1,0:T(8,128)(2,1)}, bf16[800,512]{1,0:T(8,128)(2,1)S(1)}, u32[]{:S(2)}, u32[]{:S(2)}) collective-permute-start(bf16[800,512]{1,0:T(8,128)(2,1)} %get-tuple-element.122), channel_id=1, source_target_pairs={{0,5},{1,4},{2,7},{3,6},{4,1},{5,0},{6,3},{7,2},{8,13},{9,12},{10,... | collective-permute-start | bytes 2457608 | tf_op jit(solution)/shard_map/ppermute | solution.py:56
  322.9 56.2 %collective-permute-start.23 = (bf16[800,512]{1,0:T(8,128)(2,1)S(1)}, bf16[800,512]{1,0:T(8,128)(2,1)S(1)}, u32[]{:S(2)}, u32[]{:S(2)}) collective-permute-start(bf16[800,512]{1,0:T(8,128)(2,1)S(1)} %copy-done.6), channel_id=1, source_target_pairs={{0,3},{1,2},{2,1},{3,0},{4,7},{5,6},{6,5},{7,4},{8,11},{9,10},{10,... | collective-permute-start | bytes 2457608 | tf_op jit(solution)/shard_map/ppermute | solution.py:56
  341.8 38.5 %collective-permute-start.26 = (bf16[800,512]{1,0:T(8,128)(2,1)S(1)}, bf16[800,512]{1,0:T(8,128)(2,1)S(1)}, u32[]{:S(2)}, u32[]{:S(2)}) collective-permute-start(bf16[800,512]{1,0:T(8,128)(2,1)S(1)} %copy-done.5), channel_id=1, source_target_pairs={{0,6},{1,7},{2,4},{3,5},{4,2},{5,3},{6,0},{7,1},{8,14},{9,15},{10,... | collective-permute-start | bytes 2457608 | tf_op jit(solution)/shard_map/ppermute | solution.py:56
  343.3 52.8 %collective-permute-start.24 = (bf16[800,512]{1,0:T(8,128)(2,1)S(1)}, bf16[800,512]{1,0:T(8,128)(2,1)S(1)}, u32[]{:S(2)}, u32[]{:S(2)}) collective-permute-start(bf16[800,512]{1,0:T(8,128)(2,1)S(1)} %copy-done.4), channel_id=1, source_target_pairs={{0,4},{1,5},{2,6},{3,7},{4,0},{5,1},{6,2},{7,3},{8,12},{9,13},{10,... | collective-permute-start | bytes 2457608 | tf_op jit(solution)/shard_map/ppermute | solution.py:56
  345.2 51.7 %collective-permute-start.22 = (bf16[800,512]{1,0:T(8,128)(2,1)S(1)}, bf16[800,512]{1,0:T(8,128)(2,1)S(1)}, u32[]{:S(2)}, u32[]{:S(2)}) collective-permute-start(bf16[800,512]{1,0:T(8,128)(2,1)S(1)} %copy-done.3), channel_id=1, source_target_pairs={{0,2},{1,3},{2,0},{3,1},{4,6},{5,7},{6,4},{7,5},{8,10},{9,11},{10,... | collective-permute-start | bytes 2457608 | tf_op jit(solution)/shard_map/ppermute | solution.py:56
  377.0 55.5 %collective-permute-start.11 = (bf16[160,512]{1,0:T(8,128)(2,1)}, bf16[160,512]{1,0:T(8,128)(2,1)}, u32[]{:S(2)}, u32[]{:S(2)}) collective-permute-start(bf16[160,512]{1,0:T(8,128)(2,1)} %get-tuple-element.105), channel_id=1, source_target_pairs={{0,5},{1,4},{2,7},{3,6},{4,1},{5,0},{6,3},{7,2},{8,13},{9,12},{10,... | collective-permute-start | bytes 491528 | tf_op jit(solution)/shard_map/ppermute | solution.py:56
  379.1 53.4 %collective-permute-start.10 = (bf16[160,512]{1,0:T(8,128)(2,1)}, bf16[160,512]{1,0:T(8,128)(2,1)}, u32[]{:S(2)}, u32[]{:S(2)}) collective-permute-start(bf16[160,512]{1,0:T(8,128)(2,1)} %get-tuple-element.106), channel_id=1, source_target_pairs={{0,4},{1,5},{2,6},{3,7},{4,0},{5,1},{6,2},{7,3},{8,12},{9,13},{10,... | collective-permute-start | bytes 491528 | tf_op jit(solution)/shard_map/ppermute | solution.py:56
  380.3 52.1 %collective-permute-start.9 = (bf16[160,512]{1,0:T(8,128)(2,1)}, bf16[160,512]{1,0:T(8,128)(2,1)S(1)}, u32[]{:S(2)}, u32[]{:S(2)}) collective-permute-start(bf16[160,512]{1,0:T(8,128)(2,1)} %get-tuple-element.107), channel_id=1, source_target_pairs={{0,3},{1,2},{2,1},{3,0},{4,7},{5,6},{6,5},{7,4},{8,11},{9,10},{10,... | collective-permute-start | bytes 491528 | tf_op jit(solution)/shard_map/ppermute | solution.py:56
  (72 other events, 2453.4 us)
